TPU v7x, 32 devices: a whole 2x2x4 slice. The times are simulated.
32 devices in a mesh: seq: 16 (over z, y, x), head: 2 (over core).
Axes of the slice: x: 2, y: 2, z: 4, core: 2. Of those that a mesh axis runs over, the one named last changes fastest.
Arguments:
- hidden_state: bfloat16 [8, 4096], replicated, may hold values from -18 to 18
- query_weight: bfloat16 [4096, 2, 2048], P('seq', 'head'), may hold values from -1 to 1
- up_key: bfloat16 [2, 256, 512], P('head'), may hold values from -1 to 1
- up_value: bfloat16 [2, 256, 512], P('head'), may hold values from -0.375 to 0.375
- latent_key: bfloat16 [8, 16384, 2, 256], P(None, 'seq', 'head'), may hold values from -256 to 256
- latent_value: bfloat16 [8, 16384, 2, 256], P(None, 'seq', 'head'), may hold values from -6 to 6
- lengths: int32 [8], replicated, may hold values from 12288 to 16384
- block_mask: int32 [8, 64], P(None, 'seq'), may hold values from 0 to 1, as said below
- out_weight: bfloat16 [2, 2048, 4096], P('head', 'seq'), may hold values from -0.09375 to 0.09375
Outputs:
- attn_out: float32 [8, 4096], replicated
Inputs may be any that keep to these rules, and one draw needn't show every extreme that they name: `block_mask`: blocks 0 and 32 of every sequence are valid.
All inputs are finite; a program needn't handle non-finite values.
Results may differ from a plain program's by a relative error of at most 0.0035.
Values sent between devices are 32-bit elements; how exact they have to be, the bound alone decides.
A program may use at most 64 MiB of HBM per device.

v0:
```python
import math

import jax
import jax.numpy as jnp
from jax import lax
from jax.sharding import PartitionSpec as P

HD = 128
R = 256
BLOCK = 256
KPG = 4
REP = 4
QW = 2048


def joined(part, axis, combine):
    gathered = jax.tree.map(lambda a: lax.all_gather(a, axis), part)

    def take(source):
        return jax.tree.map(lambda a: lax.dynamic_index_in_dim(a, source, 0, False), gathered)

    return lax.fori_loop(
        1, lax.axis_size(axis), lambda source, state: combine(state, take(source)), take(0)
    )


def join_carries(earlier, later):
    peak_a, total_a, summed_a = earlier
    peak_b, total_b, summed_b = later
    peak = jnp.maximum(peak_a, peak_b)
    factor_a = jnp.exp(peak_a - peak)
    factor_b = jnp.exp(peak_b - peak)
    total = total_a * factor_a + total_b * factor_b
    summed = summed_a * factor_a[..., None] + summed_b * factor_b[..., None]
    return (peak, total, summed)


def body(
    hidden_state,
    query_weight,
    up_key,
    up_value,
    latent_key,
    latent_value,
    lengths,
    block_mask,
    out_weight,
):
    highest = lax.Precision.HIGHEST
    seq_index = lax.axis_index("seq")
    batch = hidden_state.shape[0]
    dim_rows = query_weight.shape[0]
    state_rows = lax.dynamic_slice_in_dim(hidden_state, seq_index * dim_rows, dim_rows, 1)
    partial_query = jnp.dot(state_rows, query_weight[:, 0, :], preferred_element_type=jnp.float32)
    query = lax.psum(partial_query, "seq")
    query_heads = query.reshape(batch, KPG, REP, HD)
    keys_lat = latent_key[:, :, 0, :]
    values_lat = latent_value[:, :, 0, :]
    context_len = keys_lat.shape[1]
    positions = seq_index * context_len + jnp.arange(context_len, dtype=jnp.int32)
    block_full = jnp.repeat(block_mask, BLOCK, axis=1)
    valid = (positions[None, :] < lengths[:, None]) & (block_full > 0)
    mask_heads = valid[:, None, None, :]
    scale = 1.0 / math.sqrt(HD)
    key_maps = up_key[0].astype(jnp.float32).reshape(R, KPG, HD)
    query_latent = jnp.einsum("bjrd,ejd->bjre", query_heads, key_maps, precision=highest)
    scores = (
        jnp.einsum("bjre,bce->bjrc", query_latent, keys_lat.astype(jnp.float32), precision=highest)
        * scale
    )
    peak = jnp.max(jnp.where(mask_heads, scores, -1e30), axis=-1)
    weights = jnp.where(mask_heads, jnp.exp(scores - peak[..., None]), 0.0)
    total = jnp.sum(weights, axis=-1)
    value_maps = up_value[0].astype(jnp.float32).reshape(R, KPG, HD)
    latent_sum = jnp.einsum(
        "bjrc,bce->bjre", weights, values_lat.astype(jnp.float32), precision=highest
    )
    summed = jnp.einsum("bjre,ejd->bjrd", latent_sum, value_maps, precision=highest)
    out_rows = out_weight.shape[1]
    peak_all, total_all, summed_all = joined((peak, total, summed), "seq", join_carries)
    context = (summed_all / total_all[..., None]).reshape(batch, QW).astype(jnp.bfloat16)
    context_rows = lax.dynamic_slice_in_dim(context, seq_index * out_rows, out_rows, 1)
    partial_out = jnp.dot(context_rows, out_weight[0], preferred_element_type=jnp.float32)
    return lax.psum(partial_out, ("seq", "head"))


def solution(mesh):
    in_specs = (
        P(),
        P("seq", "head", None),
        P("head", None, None),
        P("head", None, None),
        P(None, "seq", "head", None),
        P(None, "seq", "head", None),
        P(),
        P(None, "seq"),
        P("head", "seq", None),
    )
    out_specs = P()
    return jax.shard_map(body, mesh=mesh, in_specs=in_specs, out_specs=out_specs, check_vma=False)
```

profile of v0, /device:TPU:1, one launch (start us, length us, event | category | flops | bytes accessed | tf_op | source)
XLA Modules:
  0.0 359.6 jit_solution(18013315302296954894)
XLA Ops:
  6.5 1.6 fusion.13
  8.1 0.7 copy.28
  8.8 0.7 broadcast_compare_fusion
  9.6 0.7 compare_and_fusion
  10.3 1.0 reshape.54
  11.4 1.0 reshape.55
  12.4 104.2 %all-reduce.3.cloned.1.call-done = f32[8,4,4,128]{3,2,1,0:T(4,128)} async-done(((f32[8,4,4,128]{3,2,1,0:T(4,128)}), f32[8,4,4,128]{3,2,1,0:T(4,128)}) %all-reduce.3.cloned.1.call-update) | async-done | bytes 65552 | tf_op jit(solution)/shard_map/psum | solution.py:55
  116.5 1.4 convolution_bitcast_fusion
  117.9 5.7 %select_reduce_fusion = (f32[8,4,4]{2,1,0:T(4,128)S(1)}, f32[8,4,4,1024]{3,2,1,0:T(4,128)S(1)}) fusion(pred[8,1024]{1,0:T(8,128)(4,1)S(1)} %compare_and_fusion, f32[8,4,4,256]{3,2,1,0:T(4,128)S(1)} %convolution_bitcast_fusion, bf16[8,1024,1,256]{3,1,2,0:T(8,128)(2,1)} %param.15), kind=kOutput, calls=%fused_computation.22 | convolution fusion | flops 403046272 | bytes 4858368 | tf_op jit(solution)/shard_map/bjre,bce->bjrc/dot_general | solution.py:68
  123.6 2.1 fusion.4
  125.7 0.9 convolution_bitcast_fusion.1
  126.7 33.3 %all-gather = f32[128,4,4]{2,1,0:T(4,128)S(1)} all-gather(f32[8,4,4]{2,1,0:T(4,128)S(1)} %get-tuple-element.223), channel_id=2, replica_groups=mesh['seq'=16,'head'=2] {'seq'}, dimensions={0}, use_global_device_ids=true | all-gather | bytes 8704 | tf_op jit(solution)/shard_map/all_gather | solution.py:17
  160.0 0.1 copy.34
  160.1 0.5 copy.37
  160.6 0.4 fusion.15
  161.0 31.0 %all-gather.1 = f32[128,4,4]{2,1,0:T(4,128)S(1)} all-gather(f32[8,4,4]{2,1,0:T(4,128)S(1)} %fusion.15), channel_id=3, replica_groups=mesh['seq'=16,'head'=2] {'seq'}, dimensions={0}, use_global_device_ids=true | all-gather | bytes 8704 | tf_op jit(solution)/shard_map/all_gather | solution.py:17
  192.0 0.1 copy.35
  192.1 0.5 copy.38
  192.6 0.8 slice.8
  193.4 20.1 %while.19 = (s32[]{:T(128)}, f32[8,4,4]{0,2,1:T(4,128)S(1)}, f32[8,4,4]{0,2,1:T(4,128)S(1)}, f32[8,4,4,128]{3,2,1,0:T(4,128)S(1)}, f32[16,8,4,4]{1,3,2,0:T(4,128...) while((s32[]{:T(128)}, f32[8,4,4]{0,2,1:T(4,128)S(1)}, ...), condition=%wide.region_4.5_spmd, body=%wide.region_3.4_spmd.sunk | while | flops 49925 | bytes 334991 | solution.py:22
  193.5 0.1 copy.68
  193.7 0.8 constant_dynamic-slice_fusion.2
  194.6 0.2 fusion.34
  194.8 0.1 copy.68
  195.0 0.8 constant_dynamic-slice_fusion.2
  195.9 0.2 fusion.34
  196.2 0.1 copy.68
  196.4 0.8 constant_dynamic-slice_fusion.2
  197.2 0.2 fusion.34
  197.5 0.1 copy.68
  197.7 0.8 constant_dynamic-slice_fusion.2
  198.6 0.2 fusion.34
  198.9 0.1 copy.68
  199.1 0.8 constant_dynamic-slice_fusion.2
  199.9 0.2 fusion.34
  200.2 0.1 copy.68
  200.4 0.8 constant_dynamic-slice_fusion.2
  201.2 0.2 fusion.34
  201.5 0.1 copy.68
  201.7 0.8 constant_dynamic-slice_fusion.2
  202.6 0.2 fusion.34
  202.9 0.1 copy.68
  203.1 0.8 constant_dynamic-slice_fusion.2
  203.9 0.2 fusion.34
  204.4 0.8 constant_dynamic-slice_fusion.2
  205.3 0.2 fusion.34
  205.5 0.1 copy.68
  205.8 0.8 constant_dynamic-slice_fusion.2
  206.6 0.2 fusion.34
  207.1 0.8 constant_dynamic-slice_fusion.2
  207.9 0.2 fusion.34
  208.4 0.8 constant_dynamic-slice_fusion.2
  209.3 0.2 fusion.34
  209.6 0.1 copy.68
  209.8 0.8 constant_dynamic-slice_fusion.2
  210.6 0.2 fusion.34
  211.1 0.8 constant_dynamic-slice_fusion.2
  212.0 0.2 fusion.34
  212.5 0.8 constant_dynamic-slice_fusion.2
  213.3 0.2 fusion.34
  213.6 0.1 divide_convert_fusion
  213.8 0.9 fusion.11
  214.7 136.8 %all-reduce.5.cloned.1.call-done = f32[8,4096]{1,0:T(8,128)} async-done(((f32[8,4096]{1,0:T(8,128)}), f32[8,4096]{1,0:T(8,128)}) %all-reduce.5.cloned.1.call-update) | async-done | bytes 131088 | tf_op jit(solution)/shard_map/psum | solution.py:84
  351.5 1.6 copy.84
  (53 shorter events, 2.9 us)
Async XLA Ops:
  6.5 207.3 %copy-start = (bf16[1,128,4096]{2,1,0:T(8,128)(2,1)S(1)}, bf16[1,128,4096]{2,1,0:T(8,128)(2,1)}, u32[]{:S(2)}) copy-start(bf16[1,128,4096]{2,1,0:T(8,128)(2,1)} %param.19) | copy-start | bytes 3145732
  6.5 110.0 %all-reduce.3.cloned.1.call-start = ((), (), s32[]{:S(2)}) async-start(), calls=%async_computation | async-start | bytes 131072 | tf_op jit(solution)/shard_map/psum | solution.py:55
  8.8 183.8 %all-gather.5.cloned.1.call-start = ((), (), s32[]{:S(2)}) async-start(), calls=%async_computation.2 | async-start | bytes 1114112 | tf_op jit(solution)/shard_map/all_gather | solution.py:17
  116.5 7.0 %copy-start.1 = (bf16[8,1024,1,256]{3,1,2,0:T(8,128)(2,1)S(1)}, bf16[8,1024,1,256]{3,1,2,0:T(8,128)(2,1)}, u32[]{:S(2)}) copy-start(bf16[8,1024,1,256]{3,1,2,0:T(8,128)(2,1)} %param.16) | copy-start | bytes 12582916
  126.6 224.9 %all-reduce.5.cloned.1.call-start = ((), (), s32[]{:S(2)}) async-start(), calls=%async_computation.1 | async-start | bytes 262144 | tf_op jit(solution)/shard_map/psum | solution.py:84
Sparse Core Ops, SparseCore 0:
  12.8 103.6 all-reduce.2
  126.8 55.3 all-gather.4
  214.9 136.5 all-reduce.4
where the time goes:
time: 362 us; the launch traced here: 360 us
  waiting for transfers between devices  241 us (67%)
  blocking collectives  64.3 us (18%)
  local copies, waits for them, and re-layouts  22.3 us (6%)
  between operations  13.2 us (4%)
  matrix products  12.6 us (3%)
  other arithmetic  5.91 us (2%)
    psum x1, waiting for transfers between devices, body(): return lax.psum(partial_out, ('seq', 'head'))  137 us
    psum x1, waiting for transfers between devices, body(): query = lax.psum(partial_query, 'seq')  104 us
    all_gather x2, blocking collectives, joined(): gathered = jax.tree.map(lambda a: lax.all_gather(a, axis), part)  64.3 us
    dynamic_slice x18, local copies, waits for them, and re-layouts, take(): lax.dynamic_index_in_dim(a, source, 0, False)  13.5 us
  transfers between devices with their start and end apart: 3, of which 2 were waited for; matrix products, arithmetic and copies ran while one was open for 1% of the time, Pallas kernels for 0%

commit v1 on v0

v1 whole, which is shorter than its diff:
```python
import functools
import math

import jax
import jax.numpy as jnp
from jax import lax
from jax.experimental import pallas as pl
from jax.experimental.pallas import tpu as pltpu
from jax.sharding import PartitionSpec as P

HD = 128
BLOCK = 256
KPG = 4
REP = 4
MESH = pl.DeviceIdType.MESH
NEG = -1e30


def repeat(count, step):
    if count <= 32:
        for i in range(count):
            step(i)
    else:
        lax.fori_loop(0, count, lambda i, c: (step(i), c)[1], 0)


def halves(x):
    high = x.astype(jnp.bfloat16)
    low = (x - high.astype(jnp.float32)).astype(jnp.bfloat16)
    return jnp.concatenate([high, low], axis=0)


def dot_nt(a, b):
    return lax.dot_general(a, b, (((1,), (1,)), ((), ())), preferred_element_type=jnp.float32)


def strided(ref, first, count, stride):
    parts = [ref[k, pl.ds(first, count, stride=stride), :] for k in range(ref.shape[0])]
    return jnp.concatenate(parts, axis=1)


def folded(x):
    rows = x.shape[0] // 2
    return x[:rows] + x[rows:]


def kernel(
    n,
    cores,
    lengths,
    block_mask,
    hidden,
    query_weight,
    up_key,
    up_value,
    keys,
    values,
    out_weight,
    out,
    qw,
    uk,
    uv,
    kv,
    vv,
    ow,
    send1,
    recv1,
    send2,
    recv2,
    ql,
    ls,
    st,
    send3,
    recv3,
    send4,
    recv4,
    send5,
    recv5,
    load_sem,
    key_sem,
    value_sem,
    send_sem,
    recv_sem,
):
    me = lax.axis_index("seq")
    core = lax.axis_index("head")
    batch, context_len = keys.shape[0], keys.shape[1]
    heads = KPG * REP
    spread = n // heads
    my_head = me // spread
    chunks = out.shape[1] // HD
    per_head = chunks // heads
    my_chunk = my_head * per_head + core
    dim_rows, out_rows = query_weight.shape[0], out_weight.shape[0]
    owner = lax.rem(me, spread) == 0

    def local(src, dst, sem):
        return pltpu.make_async_copy(src, dst, sem)

    def remote(src, dst, phase, seq, head):
        return pltpu.make_async_remote_copy(
            src_ref=src,
            dst_ref=dst,
            send_sem=send_sem.at[phase],
            recv_sem=recv_sem.at[phase],
            device_id=(seq, head),
            device_id_type=MESH,
        )

    def to_either(here, src, dst, phase, seq, head):
        if here is True:
            local(src, dst, recv_sem.at[phase]).start()
        elif here is False:
            remote(src, dst, phase, seq, head).start()
        else:

            @pl.when(here)
            def _():
                local(src, dst, recv_sem.at[phase]).start()

            @pl.when(jnp.logical_not(here))
            def _():
                remote(src, dst, phase, seq, head).start()

    def wait_bytes(ref, sem):
        local(ref, ref, sem).wait()

    def when_owner(action):
        if spread == 1:
            action()
        else:
            pl.when(owner)(action)

    def first_is_here():
        return True if spread == 1 else owner

    if dim_rows >= HD:
        qw_at = qw
    else:
        qw_at = qw.at[pl.ds(pl.multiple_of(lax.rem(me * dim_rows, HD), dim_rows), dim_rows)]
    qw_copy = local(query_weight, qw_at, load_sem.at[0])
    qw_copy.start()

    barrier = pltpu.get_barrier_semaphore()
    devices = n * cores

    def greet(i):
        other = lax.rem(me * cores + core + i + 1, devices)
        pl.semaphore_signal(
            barrier, inc=1, device_id=(other // cores, lax.rem(other, cores)), device_id_type=MESH
        )

    repeat(devices - 1, greet)

    qw_copy.wait()
    uk_copy = local(up_key, uk, load_sem.at[1])
    uk_copy.start()
    key_copies = [local(keys.at[b], kv.at[b], key_sem.at[b]) for b in range(batch)]
    value_copies = [local(values.at[b], vv.at[b], value_sem.at[b]) for b in range(batch)]
    for b in range(batch):
        key_copies[b].start()
        value_copies[b].start()
    uv_copy = local(up_value, uv, load_sem.at[2])
    uv_copy.start()
    if out_rows >= HD:
        ow_at = ow
    else:
        ow_at = ow.at[pl.ds(pl.multiple_of(lax.rem(me * out_rows, HD), out_rows), out_rows)]
    ow_copy = local(out_weight, ow_at, load_sem.at[3])
    ow_copy.start()

    if dim_rows >= HD:
        state = hidden[:, pl.ds(pl.multiple_of(me * dim_rows, HD), dim_rows)]
        weight = qw[...]
    else:
        start = lax.rem(me * dim_rows, HD)
        state = hidden[:, pl.ds(pl.multiple_of(me * dim_rows - start, HD), HD)]
        row = lax.broadcasted_iota(jnp.int32, qw.shape, 0)
        weight = jnp.where((row >= start) & (row < start + dim_rows), qw[...].astype(jnp.float32), 0.0)
        weight = weight.astype(jnp.bfloat16)
    part = jnp.dot(state, weight, preferred_element_type=jnp.float32)
    for h in range(heads):
        send1[h] = part[:, h * HD : (h + 1) * HD]

    pl.semaphore_wait(barrier, devices - 1)

    for i in range(heads):
        h = lax.rem(my_head + i, heads)
        here = first_is_here() if i == 0 else False
        to_either(here, send1.at[h], recv1.at[me], 0, h * spread, core)

    def gather_query():
        wait_bytes(recv1, recv_sem.at[0])
        send2[...] = jnp.sum(recv1[...], axis=0)
        local(send2, recv2.at[my_head], recv_sem.at[1]).start()

        def send(i):
            remote(send2, recv2.at[my_head], 1, lax.rem(me + i + 1, n), core).start()

        repeat(n - 1, send)

    when_owner(gather_query)
    uk_copy.wait()
    wait_bytes(recv2, recv_sem.at[1])

    scale = 1.0 / math.sqrt(HD)
    rank = uk.shape[0]
    for j in range(KPG):
        rows = recv2[j * REP : (j + 1) * REP].reshape(REP * batch, HD)
        mapped = folded(dot_nt(halves(rows), uk[:, j * HD : (j + 1) * HD])) * scale
        for k in range(rank // HD):
            ql[k, j * REP * batch : (j + 1) * REP * batch, :] = mapped[:, k * HD : (k + 1) * HD]

    blocks = context_len // BLOCK
    lane = lax.broadcasted_iota(jnp.int32, (1, BLOCK), 1)
    stat_lane = lax.broadcasted_iota(jnp.int32, (heads, HD), 1)
    for b in range(batch):
        query = halves(strided(ql, b, heads, batch))
        key_copies[b].wait()
        scores = folded(dot_nt(query, kv[b]))
        limits = [
            jnp.where(block_mask[k, b] == 1, lengths[b] - me * context_len - k * BLOCK, 0)
            for k in range(blocks)
        ]
        valid = jnp.concatenate([lane < limit for limit in limits], axis=1)
        scores = jnp.where(valid, scores, NEG)
        peak = jnp.max(scores, axis=1, keepdims=True)
        weights = jnp.where(valid, jnp.exp(scores - peak), 0.0)
        total = jnp.sum(weights, axis=1, keepdims=True)
        value_copies[b].wait()
        latent = folded(jnp.dot(halves(weights), vv[b], preferred_element_type=jnp.float32))
        for k in range(rank // HD):
            ls[k, b * heads : (b + 1) * heads, :] = latent[:, k * HD : (k + 1) * HD]
        st[b * heads : (b + 1) * heads, :] = jnp.where(stat_lane < HD // 2, peak, total)

    uv_copy.wait()
    for j in range(KPG):
        rows = jnp.concatenate(
            [strided(ls, j * REP + r, batch, heads) for r in range(REP)], axis=0
        )
        summed = folded(
            jnp.dot(halves(rows), uv[:, j * HD : (j + 1) * HD], preferred_element_type=jnp.float32)
        )
        for r in range(REP):
            h = j * REP + r
            send3[h, 0:batch] = summed[r * batch : (r + 1) * batch]
            send3[h, batch : 2 * batch] = st[pl.ds(h, batch, stride=heads), :]

    local(send3.at[my_head], recv3.at[me], recv_sem.at[2]).start()

    def send_carry(i):
        target = lax.rem(me + i + 1, n)
        remote(send3.at[target // spread], recv3.at[me], 2, target, core).start()

    repeat(n - 1, send_carry)
    wait_bytes(recv3, recv_sem.at[2])

    stats = recv3[:, batch : 2 * batch, :]
    turned = pltpu.roll(stats, HD // 2, 2)
    low_lanes = lax.broadcasted_iota(jnp.int32, stats.shape, 2) < HD // 2
    peaks = jnp.where(low_lanes, stats, turned)
    totals = jnp.where(low_lanes, turned, stats)
    factor = jnp.exp(peaks - jnp.max(peaks, axis=0, keepdims=True))
    summed = jnp.sum(recv3[:, 0:batch, :] * factor, axis=0)
    context = (summed / jnp.sum(totals * factor, axis=0)).astype(jnp.bfloat16)

    ow_copy.wait()
    if out_rows >= HD:
        weight = ow[...]
    else:
        start = lax.rem(me * out_rows, HD)
        row = lax.broadcasted_iota(jnp.int32, ow.shape, 0)
        weight = jnp.where((row >= start) & (row < start + out_rows), ow[...].astype(jnp.float32), 0.0)
        weight = weight.astype(jnp.bfloat16)
    part = jnp.dot(context, weight, preferred_element_type=jnp.float32)
    for c in range(chunks):
        send4[c] = part[:, c * HD : (c + 1) * HD]

    for i in range(chunks):
        c = lax.rem(my_chunk + i, chunks)
        here = first_is_here() if i == 0 else False
        to_either(here, send4.at[c], recv4.at[me * cores + core], 3, c // per_head * spread, lax.rem(c, per_head))

    def gather_out():
        wait_bytes(recv4, recv_sem.at[3])
        send5[...] = jnp.sum(recv4[...], axis=0)
        local(send5, recv5.at[my_chunk], recv_sem.at[4]).start()

        def send(i):
            other = lax.rem(me * cores + core + i + 1, devices)
            remote(send5, recv5.at[my_chunk], 4, other // cores, lax.rem(other, cores)).start()

        repeat(devices - 1, send)

    when_owner(gather_out)
    wait_bytes(recv5, recv_sem.at[4])
    for c in range(chunks):
        out[:, c * HD : (c + 1) * HD] = recv5[c]

    def owner_sends():
        wait_bytes(send1.at[pl.ds(0, heads - 1)], send_sem.at[0])
        wait_bytes(recv1.at[pl.ds(0, n - 1)], send_sem.at[1])
        wait_bytes(send4.at[pl.ds(0, chunks - 1)], send_sem.at[3])
        wait_bytes(recv4.at[pl.ds(0, devices - 1)], send_sem.at[4])

    when_owner(owner_sends)
    if spread > 1:

        @pl.when(jnp.logical_not(owner))
        def _():
            wait_bytes(send1, send_sem.at[0])
            wait_bytes(send4, send_sem.at[3])

    wait_bytes(recv3.at[pl.ds(0, n - 1)], send_sem.at[2])


def body(
    n,
    cores,
    hidden_state,
    query_weight,
    up_key,
    up_value,
    latent_key,
    latent_value,
    lengths,
    block_mask,
    out_weight,
):
    batch, context_len, _, rank = latent_key.shape
    width = query_weight.shape[2]
    heads = KPG * REP
    model = out_weight.shape[2]
    chunks = model // HD
    f32, bf16 = jnp.float32, jnp.bfloat16
    vmem = pltpu.VMEM
    return pl.pallas_call(
        functools.partial(kernel, n, cores),
        out_shape=jax.ShapeDtypeStruct((batch, model), f32),
        in_specs=[pl.BlockSpec(memory_space=pltpu.SMEM)] * 2
        + [pl.BlockSpec(memory_space=pltpu.VMEM)]
        + [pl.BlockSpec(memory_space=pl.ANY)] * 6,
        out_specs=pl.BlockSpec(memory_space=pltpu.VMEM),
        scratch_shapes=[
            vmem((max(query_weight.shape[0], HD), width), bf16),
            vmem(up_key.shape[1:], bf16),
            vmem(up_value.shape[1:], bf16),
            vmem((batch, context_len, rank), bf16),
            vmem((batch, context_len, rank), bf16),
            vmem((max(out_weight.shape[1], HD), model), bf16),
            vmem((heads, batch, HD), f32),
            vmem((n, batch, HD), f32),
            vmem((batch, HD), f32),
            vmem((heads, batch, HD), f32),
            vmem((rank // HD, heads * batch, HD), f32),
            vmem((rank // HD, heads * batch, HD), f32),
            vmem((heads * batch, HD), f32),
            vmem((heads, 2 * batch, HD), f32),
            vmem((n, 2 * batch, HD), f32),
            vmem((chunks, batch, HD), f32),
            vmem((n * cores, batch, HD), f32),
            vmem((batch, HD), f32),
            vmem((chunks, batch, HD), f32),
            pltpu.SemaphoreType.DMA((4,)),
            pltpu.SemaphoreType.DMA((batch,)),
            pltpu.SemaphoreType.DMA((batch,)),
            pltpu.SemaphoreType.DMA((5,)),
            pltpu.SemaphoreType.DMA((5,)),
        ],
        compiler_params=pltpu.CompilerParams(collective_id=0, has_side_effects=True),
    )(
        lengths,
        block_mask.T,
        hidden_state,
        query_weight.reshape(query_weight.shape[0], width),
        up_key.reshape(up_key.shape[1:]),
        up_value.reshape(up_value.shape[1:]),
        latent_key.reshape(batch, context_len, rank),
        latent_value.reshape(batch, context_len, rank),
        out_weight.reshape(out_weight.shape[1:]),
    )


def solution(mesh):
    in_specs = (
        P(),
        P("seq", "head", None),
        P("head", None, None),
        P("head", None, None),
        P(None, "seq", "head", None),
        P(None, "seq", "head", None),
        P(),
        P(None, "seq"),
        P("head", "seq", None),
    )
    return jax.shard_map(
        functools.partial(body, mesh.shape["seq"], mesh.shape["head"]),
        mesh=mesh,
        in_specs=in_specs,
        out_specs=P(),
        check_vma=False,
    )
```

time: 362 us -> 40.4 us (0.11)
  waiting for transfers between devices: 241 us -> 0 us
  blocking collectives: 64.3 us -> 0 us
  Pallas kernels: 0 us -> 38.2 us
  local copies, waits for them, and re-layouts: 22.3 us -> 1.57 us
  between operations: 13.2 us -> 0.01 us
  matrix products: 12.6 us -> 0 us
  other arithmetic: 5.91 us -> 0 us
    psum x2 -> x0, waiting for transfers between devices: 241 us -> none  [the longest x1 137 us: body(): return lax.psum(partial_out, ('seq', 'head'))]
    all_gather x2 -> x0, blocking collectives: 64.3 us -> none  [joined(): gathered = jax.tree.map(lambda a: lax.all_gather(a, axis), part)]
    pallas_call x0 -> x1, Pallas kernels: none -> 38.2 us  [body(): pl.pallas_call(functools.partial(kernel, n, cores), out_shape=jax.ShapeDt...]
    dynamic_slice x18 -> x0, local copies, waits for them, and re-layouts: 13.5 us -> none  [take(): lax.dynamic_index_in_dim(a, source, 0, False)]
    dot_general x6 -> x0, matrix products: 12.6 us -> none  [the longest x1 5.67 us: body(): jnp.einsum('bjre,bce->bjrc', query_latent, keys_lat.astype(jnp.float32),...]
    add x31 -> x0, other arithmetic: 3.96 us -> none  [the longest x15 3.51 us: join_carries(): summed = summed_a * factor_a[..., None] + summed_b * factor_b[..., None]]
  transfers between devices with their start and end apart: 3 -> 0, of which waited for: 2 -> 0; matrix products, arithmetic and copies ran while one was open for 1% -> 0% of each run, Pallas kernels for 0% -> 0%
where the time goes in v1:
time: 40.4 us; the launch traced here: 39.8 us
  Pallas kernels  38.2 us (95%)
  local copies, waits for them, and re-layouts  1.57 us (4%)
    pallas_call x1, Pallas kernels, body(): pl.pallas_call(functools.partial(kernel, n, cores), out_shape=jax.ShapeDt...  38.2 us
    unnamed x1, local copies, waits for them, and re-layouts  1.57 us

profile of v1, /device:TPU:1, one launch (start us, length us, event | category | flops | bytes accessed | tf_op | source)
XLA Modules:
  0.0 39.8 jit_solution(12211695449863263682)
XLA Ops:
  0.0 38.2 %shard_map.91 = f32[8,4096]{1,0:T(8,128)} custom-call(s32[8]{0:T(128)} %lengths.1, s32[4,8]{1,0:T(4,128)} %bitcast.13, bf16[8,4096]{1,0:T(8,128)(2,1)} %hidden.1, bf16[256,2048]{1,0:T(8,128)(2,1)} %bitcast.9, bf16[256,512]{1,0:T(8,128)(2,1)} %bitcast.11, bf16[256,512]{1,0:T(8,128)(2,1)} %bitcast.12, bf16[8,1024,256]{2,1,0:T(8,128)(2,1)} %bitcast.7, ...), custom_call_target="tpu_custom_call" | custom-call | tf_op jit(solution)/shard_map/pallas_call | solution.py:337
  38.2 1.6 %copy.11 = f32[8,4096]{1,0:T(8,128)} copy(f32[8,4096]{1,0:T(8,128)} %shard_map.91) | data formatting | bytes 262144

commit v2 on v1

--- a/solution.py
+++ b/solution.py
@@ -16,12 +16,13 @@
 NEG = -1e30
 
 
-def repeat(count, step):
-    if count <= 32:
-        for i in range(count):
-            step(i)
+def each_other(me, count, step):
+    if count <= 32 and count & (count - 1) == 0:
+        flips = [(1 << b) * (1 - 2 * lax.rem(me // (1 << b), 2)) for b in range(count.bit_length() - 1)]
+        for mask in reversed(range(1, count)):
+            step(me + sum(flip for b, flip in enumerate(flips) if mask >> b & 1))
     else:
-        lax.fori_loop(0, count, lambda i, c: (step(i), c)[1], 0)
+        lax.fori_loop(0, count - 1, lambda i, c: (step(lax.rem(me + i + 1, count)), c)[1], 0)
 
 
 def halves(x):
@@ -47,9 +48,9 @@
 def kernel(
     n,
     cores,
-    lengths,
-    block_mask,
-    hidden,
+    lengths_in,
+    mask_in,
+    hidden_in,
     query_weight,
     up_key,
     up_value,
@@ -57,6 +58,9 @@
     values,
     out_weight,
     out,
+    lengths,
+    block_mask,
+    hidden,
     qw,
     uk,
     uv,
@@ -76,6 +80,11 @@
     recv4,
     send5,
     recv5,
+    send6,
+    recv6,
+    send7,
+    recv7,
+    pw,
     load_sem,
     key_sem,
     value_sem,
@@ -89,8 +98,7 @@
     spread = n // heads
     my_head = me // spread
     chunks = out.shape[1] // HD
-    per_head = chunks // heads
-    my_chunk = my_head * per_head + core
+    my_chunk = core * heads + my_head
     dim_rows, out_rows = query_weight.shape[0], out_weight.shape[0]
     owner = lax.rem(me, spread) == 0
 
@@ -139,20 +147,26 @@
     else:
         qw_at = qw.at[pl.ds(pl.multiple_of(lax.rem(me * dim_rows, HD), dim_rows), dim_rows)]
     qw_copy = local(query_weight, qw_at, load_sem.at[0])
+    hidden_copy = local(hidden_in, hidden, load_sem.at[4])
+    hidden_copy.start()
     qw_copy.start()
 
     barrier = pltpu.get_barrier_semaphore()
     devices = n * cores
 
-    def greet(i):
-        other = lax.rem(me * cores + core + i + 1, devices)
+    def greet(other):
         pl.semaphore_signal(
             barrier, inc=1, device_id=(other // cores, lax.rem(other, cores)), device_id_type=MESH
         )
 
-    repeat(devices - 1, greet)
-
+    each_other(me * cores + core, devices, greet)
+
+    hidden_copy.wait()
     qw_copy.wait()
+    lengths_copy = local(lengths_in, lengths, load_sem.at[5])
+    lengths_copy.start()
+    mask_copy = local(mask_in, block_mask, load_sem.at[6])
+    mask_copy.start()
     uk_copy = local(up_key, uk, load_sem.at[1])
     uk_copy.start()
     key_copies = [local(keys.at[b], kv.at[b], key_sem.at[b]) for b in range(batch)]
@@ -184,20 +198,21 @@
 
     pl.semaphore_wait(barrier, devices - 1)
 
-    for i in range(heads):
-        h = lax.rem(my_head + i, heads)
-        here = first_is_here() if i == 0 else False
-        to_either(here, send1.at[h], recv1.at[me], 0, h * spread, core)
+    def send_query(h):
+        remote(send1.at[h], recv1.at[me], 0, h * spread, core).start()
+
+    each_other(my_head, heads, send_query)
+    to_either(first_is_here(), send1.at[my_head], recv1.at[me], 0, my_head * spread, core)
 
     def gather_query():
         wait_bytes(recv1, recv_sem.at[0])
         send2[...] = jnp.sum(recv1[...], axis=0)
+
+        def send(other):
+            remote(send2, recv2.at[my_head], 1, other, core).start()
+
+        each_other(me, n, send)
         local(send2, recv2.at[my_head], recv_sem.at[1]).start()
-
-        def send(i):
-            remote(send2, recv2.at[my_head], 1, lax.rem(me + i + 1, n), core).start()
-
-        repeat(n - 1, send)
 
     when_owner(gather_query)
     uk_copy.wait()
@@ -211,12 +226,15 @@
         for k in range(rank // HD):
             ql[k, j * REP * batch : (j + 1) * REP * batch, :] = mapped[:, k * HD : (k + 1) * HD]
 
+    lengths_copy.wait()
+    mask_copy.wait()
     blocks = context_len // BLOCK
     lane = lax.broadcasted_iota(jnp.int32, (1, BLOCK), 1)
     stat_lane = lax.broadcasted_iota(jnp.int32, (heads, HD), 1)
     for b in range(batch):
+        key_copies[b].wait()
+    for b in range(batch):
         query = halves(strided(ql, b, heads, batch))
-        key_copies[b].wait()
         scores = folded(dot_nt(query, kv[b]))
         limits = [
             jnp.where(block_mask[k, b] == 1, lengths[b] - me * context_len - k * BLOCK, 0)
@@ -227,11 +245,23 @@
         peak = jnp.max(scores, axis=1, keepdims=True)
         weights = jnp.where(valid, jnp.exp(scores - peak), 0.0)
         total = jnp.sum(weights, axis=1, keepdims=True)
+        pw[b] = halves(weights)
+        st[b * heads : (b + 1) * heads, :] = jnp.where(stat_lane < HD // 2, peak, total)
+    for h in range(heads):
+        send6[h] = st[pl.ds(h, batch, stride=heads), :]
+
+    def send_stats(other):
+        remote(send6.at[other // spread], recv6.at[me], 5, other, core).start()
+
+    each_other(me, n, send_stats)
+    local(send6.at[my_head], recv6.at[me], recv_sem.at[5]).start()
+
+    for b in range(batch):
         value_copies[b].wait()
-        latent = folded(jnp.dot(halves(weights), vv[b], preferred_element_type=jnp.float32))
+    for b in range(batch):
+        latent = folded(jnp.dot(pw[b], vv[b], preferred_element_type=jnp.float32))
         for k in range(rank // HD):
             ls[k, b * heads : (b + 1) * heads, :] = latent[:, k * HD : (k + 1) * HD]
-        st[b * heads : (b + 1) * heads, :] = jnp.where(stat_lane < HD // 2, peak, total)
 
     uv_copy.wait()
     for j in range(KPG):
@@ -243,26 +273,26 @@
         )
         for r in range(REP):
             h = j * REP + r
-            send3[h, 0:batch] = summed[r * batch : (r + 1) * batch]
-            send3[h, batch : 2 * batch] = st[pl.ds(h, batch, stride=heads), :]
-
+            send3[h] = summed[r * batch : (r + 1) * batch]
+
+    def send_carry(other):
+        remote(send3.at[other // spread], recv3.at[me], 2, other, core).start()
+
+    each_other(me, n, send_carry)
     local(send3.at[my_head], recv3.at[me], recv_sem.at[2]).start()
 
-    def send_carry(i):
-        target = lax.rem(me + i + 1, n)
-        remote(send3.at[target // spread], recv3.at[me], 2, target, core).start()
-
-    repeat(n - 1, send_carry)
-    wait_bytes(recv3, recv_sem.at[2])
-
-    stats = recv3[:, batch : 2 * batch, :]
+    wait_bytes(recv6, recv_sem.at[5])
+    stats = recv6[...]
     turned = pltpu.roll(stats, HD // 2, 2)
     low_lanes = lax.broadcasted_iota(jnp.int32, stats.shape, 2) < HD // 2
     peaks = jnp.where(low_lanes, stats, turned)
     totals = jnp.where(low_lanes, turned, stats)
     factor = jnp.exp(peaks - jnp.max(peaks, axis=0, keepdims=True))
-    summed = jnp.sum(recv3[:, 0:batch, :] * factor, axis=0)
-    context = (summed / jnp.sum(totals * factor, axis=0)).astype(jnp.bfloat16)
+    factor = factor / jnp.sum(totals * factor, axis=0, keepdims=True)
+
+    wait_bytes(recv3, recv_sem.at[2])
+
+    context = jnp.sum(recv3[...] * factor, axis=0).astype(jnp.bfloat16)
 
     ow_copy.wait()
     if out_rows >= HD:
@@ -276,21 +306,26 @@
     for c in range(chunks):
         send4[c] = part[:, c * HD : (c + 1) * HD]
 
-    for i in range(chunks):
-        c = lax.rem(my_chunk + i, chunks)
-        here = first_is_here() if i == 0 else False
-        to_either(here, send4.at[c], recv4.at[me * cores + core], 3, c // per_head * spread, lax.rem(c, per_head))
+    half = chunks // cores
+    remote(send4.at[pl.ds((1 - core) * half, half)], recv7, 6, me, 1 - core).start()
+    wait_bytes(recv7, recv_sem.at[6])
+    send7[...] = send4[pl.ds(core * half, half)] + recv7[...]
+
+    def send_part(c):
+        remote(send7.at[c], recv4.at[me], 3, c * spread, core).start()
+
+    each_other(my_head, heads, send_part)
+    to_either(first_is_here(), send7.at[my_head], recv4.at[me], 3, my_head * spread, core)
 
     def gather_out():
         wait_bytes(recv4, recv_sem.at[3])
         send5[...] = jnp.sum(recv4[...], axis=0)
+
+        def send(other):
+            remote(send5, recv5.at[my_chunk], 4, other // cores, lax.rem(other, cores)).start()
+
+        each_other(me * cores + core, devices, send)
         local(send5, recv5.at[my_chunk], recv_sem.at[4]).start()
-
-        def send(i):
-            other = lax.rem(me * cores + core + i + 1, devices)
-            remote(send5, recv5.at[my_chunk], 4, other // cores, lax.rem(other, cores)).start()
-
-        repeat(devices - 1, send)
 
     when_owner(gather_out)
     wait_bytes(recv5, recv_sem.at[4])
@@ -300,8 +335,12 @@
     def owner_sends():
         wait_bytes(send1.at[pl.ds(0, heads - 1)], send_sem.at[0])
         wait_bytes(recv1.at[pl.ds(0, n - 1)], send_sem.at[1])
-        wait_bytes(send4.at[pl.ds(0, chunks - 1)], send_sem.at[3])
-        wait_bytes(recv4.at[pl.ds(0, devices - 1)], send_sem.at[4])
+        wait_bytes(send7.at[pl.ds(0, heads - 1)], send_sem.at[3])
+        if devices - 1 <= chunks:
+            wait_bytes(recv5.at[pl.ds(0, devices - 1)], send_sem.at[4])
+        else:
+            wait_bytes(recv4, send_sem.at[4])
+            wait_bytes(recv4.at[pl.ds(0, n - 1)], send_sem.at[4])
 
     when_owner(owner_sends)
     if spread > 1:
@@ -309,9 +348,11 @@
         @pl.when(jnp.logical_not(owner))
         def _():
             wait_bytes(send1, send_sem.at[0])
-            wait_bytes(send4, send_sem.at[3])
+            wait_bytes(send7, send_sem.at[3])
 
     wait_bytes(recv3.at[pl.ds(0, n - 1)], send_sem.at[2])
+    wait_bytes(recv6.at[pl.ds(0, n - 1)], send_sem.at[5])
+    wait_bytes(recv7, send_sem.at[6])
 
 
 def body(
@@ -337,11 +378,12 @@
     return pl.pallas_call(
         functools.partial(kernel, n, cores),
         out_shape=jax.ShapeDtypeStruct((batch, model), f32),
-        in_specs=[pl.BlockSpec(memory_space=pltpu.SMEM)] * 2
-        + [pl.BlockSpec(memory_space=pltpu.VMEM)]
-        + [pl.BlockSpec(memory_space=pl.ANY)] * 6,
+        in_specs=[pl.BlockSpec(memory_space=pl.ANY)] * 9,
         out_specs=pl.BlockSpec(memory_space=pltpu.VMEM),
         scratch_shapes=[
+            pltpu.SMEM(lengths.shape, jnp.int32),
+            pltpu.SMEM(block_mask.shape[::-1], jnp.int32),
+            vmem(hidden_state.shape, bf16),
             vmem((max(query_weight.shape[0], HD), width), bf16),
             vmem(up_key.shape[1:], bf16),
             vmem(up_value.shape[1:], bf16),
@@ -355,17 +397,22 @@
             vmem((rank // HD, heads * batch, HD), f32),
             vmem((rank // HD, heads * batch, HD), f32),
             vmem((heads * batch, HD), f32),
-            vmem((heads, 2 * batch, HD), f32),
-            vmem((n, 2 * batch, HD), f32),
+            vmem((heads, batch, HD), f32),
+            vmem((n, batch, HD), f32),
             vmem((chunks, batch, HD), f32),
-            vmem((n * cores, batch, HD), f32),
+            vmem((n, batch, HD), f32),
             vmem((batch, HD), f32),
             vmem((chunks, batch, HD), f32),
-            pltpu.SemaphoreType.DMA((4,)),
+            vmem((heads, batch, HD), f32),
+            vmem((n, batch, HD), f32),
+            vmem((chunks // cores, batch, HD), f32),
+            vmem((chunks // cores, batch, HD), f32),
+            vmem((batch, 2 * heads, context_len), bf16),
+            pltpu.SemaphoreType.DMA((7,)),
             pltpu.SemaphoreType.DMA((batch,)),
             pltpu.SemaphoreType.DMA((batch,)),
-            pltpu.SemaphoreType.DMA((5,)),
-            pltpu.SemaphoreType.DMA((5,)),
+            pltpu.SemaphoreType.DMA((7,)),
+            pltpu.SemaphoreType.DMA((7,)),
         ],
         compiler_params=pltpu.CompilerParams(collective_id=0, has_side_effects=True),
     )(

time: 40.4 us -> 35.3 us (0.87)
  Pallas kernels: 38.2 us -> 33.1 us
    pallas_call x1, Pallas kernels: 38.2 us -> 33.1 us  [body(): pl.pallas_call(functools.partial(kernel, n, cores), out_shape=jax.ShapeDt...]
where the time goes in v2:
time: 35.3 us; the launch traced here: 34.7 us
  Pallas kernels  33.1 us (94%)
  local copies, waits for them, and re-layouts  1.57 us (4%)
    pallas_call x1, Pallas kernels, body(): pl.pallas_call(functools.partial(kernel, n, cores), out_shape=jax.ShapeDt...  33.1 us
    unnamed x1, local copies, waits for them, and re-layouts  1.57 us

profile of v2, /device:TPU:1, one launch (start us, length us, event | category | flops | bytes accessed | tf_op | source)
XLA Modules:
  0.0 34.7 jit_solution(12020638939638492211)
XLA Ops:
  0.0 33.1 %shard_map.91 = f32[8,4096]{1,0:T(8,128)} custom-call(s32[8]{0:T(128)} %lengths_in.1, s32[4,8]{1,0:T(4,128)} %bitcast.13, bf16[8,4096]{1,0:T(8,128)(2,1)} %hidden_in.1, bf16[256,2048]{1,0:T(8,128)(2,1)} %bitcast.9, bf16[256,512]{1,0:T(8,128)(2,1)} %bitcast.11, bf16[256,512]{1,0:T(8,128)(2,1)} %bitcast.12, bf16[8,1024,256]{2,1,0:T(8,128)(2,1)} %bitcast.7, ...), custom_call_target="tpu_custom_call" | custom-call | tf_op jit(solution)/shard_map/pallas_call | solution.py:378
  33.1 1.6 %copy.11 = f32[8,4096]{1,0:T(8,128)} copy(f32[8,4096]{1,0:T(8,128)} %shard_map.91) | data formatting | bytes 262144

commit v3 on v2

--- a/solution.py
+++ b/solution.py
@@ -377,7 +377,7 @@
     vmem = pltpu.VMEM
     return pl.pallas_call(
         functools.partial(kernel, n, cores),
-        out_shape=jax.ShapeDtypeStruct((batch, model), f32),
+        out_shape=pltpu.VMEM((batch, model), f32),
         in_specs=[pl.BlockSpec(memory_space=pl.ANY)] * 9,
         out_specs=pl.BlockSpec(memory_space=pltpu.VMEM),
         scratch_shapes=[

time: 35.3 us -> 33.7 us (0.955)
  local copies, waits for them, and re-layouts: 1.57 us -> 0.66 us
  Pallas kernels: 33.1 us -> 32.5 us
    unnamed x1, local copies, waits for them, and re-layouts: 1.57 us -> 0.66 us
    pallas_call x1, Pallas kernels: 33.1 us -> 32.5 us  [body(): pl.pallas_call(functools.partial(kernel, n, cores), out_shape=pltpu.VMEM(...]
where the time goes in v3:
time: 33.7 us; the launch traced here: 33.1 us
  Pallas kernels  32.5 us (96%)
  local copies, waits for them, and re-layouts  0.66 us (2%)
    pallas_call x1, Pallas kernels, body(): pl.pallas_call(functools.partial(kernel, n, cores), out_shape=pltpu.VMEM(...  32.5 us

profile of v3, /device:TPU:1, one launch (start us, length us, event | category | flops | bytes accessed | tf_op | source)
XLA Modules:
  0.0 33.1 jit_solution(12268331877456697970)
XLA Ops:
  0.0 32.5 %shard_map.91 = f32[8,4096]{1,0:T(8,128)S(1)} custom-call(s32[8]{0:T(128)} %lengths_in.1, s32[4,8]{1,0:T(4,128)} %bitcast.13, bf16[8,4096]{1,0:T(8,128)(2,1)} %hidden_in.1, bf16[256,2048]{1,0:T(8,128)(2,1)} %bitcast.9, bf16[256,512]{1,0:T(8,128)(2,1)} %bitcast.11, bf16[256,512]{1,0:T(8,128)(2,1)} %bitcast.12, bf16[8,1024,256]{2,1,0:T(8,128)(2,1)} %bitcast.7, ...), custom_call_target="tpu_custom_call" | custom-call | tf_op jit(solution)/shard_map/pallas_call | solution.py:378
  32.5 0.7 %copy.11 = f32[8,4096]{1,0:T(8,128)} copy(f32[8,4096]{1,0:T(8,128)S(1)} %shard_map.91) | data formatting | bytes 262144

commit v4 on v3

--- a/solution.py
+++ b/solution.py
@@ -82,8 +82,8 @@
     recv5,
     send6,
     recv6,
-    send7,
-    recv7,
+    rows_out,
+    rows_in,
     pw,
     load_sem,
     key_sem,
@@ -97,10 +97,12 @@
     heads = KPG * REP
     spread = n // heads
     my_head = me // spread
-    chunks = out.shape[1] // HD
-    my_chunk = core * heads + my_head
+    per_head = out.shape[1] // HD // heads
+    hub = cores - 1
+    groups = recv1.shape[0]
     dim_rows, out_rows = query_weight.shape[0], out_weight.shape[0]
     owner = lax.rem(me, spread) == 0
+    is_hub = core == hub
 
     def local(src, dst, sem):
         return pltpu.make_async_copy(src, dst, sem)
@@ -115,32 +117,24 @@
             device_id_type=MESH,
         )
 
-    def to_either(here, src, dst, phase, seq, head):
-        if here is True:
-            local(src, dst, recv_sem.at[phase]).start()
-        elif here is False:
-            remote(src, dst, phase, seq, head).start()
+    def wait_bytes(ref, sem):
+        local(ref, ref, sem).wait()
+
+    def when_owner(action):
+        pl.when(is_hub if spread == 1 else is_hub & owner)(action)
+
+    def to_hub(other, own, src, dst, phase):
+        if own is None:
+            remote(src, dst, phase, other, hub).start()
         else:
 
-            @pl.when(here)
+            @pl.when(own)
             def _():
                 local(src, dst, recv_sem.at[phase]).start()
 
-            @pl.when(jnp.logical_not(here))
+            @pl.when(jnp.logical_not(own))
             def _():
-                remote(src, dst, phase, seq, head).start()
-
-    def wait_bytes(ref, sem):
-        local(ref, ref, sem).wait()
-
-    def when_owner(action):
-        if spread == 1:
-            action()
-        else:
-            pl.when(owner)(action)
-
-    def first_is_here():
-        return True if spread == 1 else owner
+                remote(src, dst, phase, other, hub).start()
 
     if dim_rows >= HD:
         qw_at = qw
@@ -150,6 +144,14 @@
     hidden_copy = local(hidden_in, hidden, load_sem.at[4])
     hidden_copy.start()
     qw_copy.start()
+
+    def output_rows():
+        if out_rows >= HD:
+            return ow[...]
+        start = lax.rem(me * out_rows, HD)
+        row = lax.broadcasted_iota(jnp.int32, ow.shape, 0)
+        kept = jnp.where((row >= start) & (row < start + out_rows), ow[...].astype(jnp.float32), 0.0)
+        return kept.astype(jnp.bfloat16)
 
     barrier = pltpu.get_barrier_semaphore()
     devices = n * cores
@@ -199,20 +201,31 @@
     pl.semaphore_wait(barrier, devices - 1)
 
     def send_query(h):
-        remote(send1.at[h], recv1.at[me], 0, h * spread, core).start()
+        to_hub(h * spread, None, send1.at[h], recv1.at[core, me], 0)
 
     each_other(my_head, heads, send_query)
-    to_either(first_is_here(), send1.at[my_head], recv1.at[me], 0, my_head * spread, core)
+    here = is_hub if spread == 1 else is_hub & owner
+    to_hub(my_head * spread, here, send1.at[my_head], recv1.at[core, me], 0)
+
+    ow_copy.wait()
+
+    @pl.when(jnp.logical_not(is_hub))
+    def _():
+        rows_out[...] = output_rows().astype(jnp.float32)
+        remote(rows_out, rows_in, 6, me, hub).start()
 
     def gather_query():
         wait_bytes(recv1, recv_sem.at[0])
-        send2[...] = jnp.sum(recv1[...], axis=0)
+        send2[...] = jnp.sum(recv1[...], axis=1)
 
         def send(other):
-            remote(send2, recv2.at[my_head], 1, other, core).start()
+            for group in range(groups):
+                remote(send2.at[group], recv2.at[my_head], 1, other, group).start()
 
         each_other(me, n, send)
-        local(send2, recv2.at[my_head], recv_sem.at[1]).start()
+        for group in range(groups - 1):
+            remote(send2.at[group], recv2.at[my_head], 1, me, group).start()
+        local(send2.at[hub], recv2.at[my_head], recv_sem.at[1]).start()
 
     when_owner(gather_query)
     uk_copy.wait()
@@ -251,10 +264,10 @@
         send6[h] = st[pl.ds(h, batch, stride=heads), :]
 
     def send_stats(other):
-        remote(send6.at[other // spread], recv6.at[me], 5, other, core).start()
+        to_hub(other, None, send6.at[other // spread], recv6.at[core, me], 5)
 
     each_other(me, n, send_stats)
-    local(send6.at[my_head], recv6.at[me], recv_sem.at[5]).start()
+    to_hub(me, is_hub, send6.at[my_head], recv6.at[core, me], 5)
 
     for b in range(batch):
         value_copies[b].wait()
@@ -276,83 +289,95 @@
             send3[h] = summed[r * batch : (r + 1) * batch]
 
     def send_carry(other):
-        remote(send3.at[other // spread], recv3.at[me], 2, other, core).start()
+        to_hub(other, None, send3.at[other // spread], recv3.at[core, me], 2)
 
     each_other(me, n, send_carry)
-    local(send3.at[my_head], recv3.at[me], recv_sem.at[2]).start()
-
-    wait_bytes(recv6, recv_sem.at[5])
-    stats = recv6[...]
-    turned = pltpu.roll(stats, HD // 2, 2)
-    low_lanes = lax.broadcasted_iota(jnp.int32, stats.shape, 2) < HD // 2
-    peaks = jnp.where(low_lanes, stats, turned)
-    totals = jnp.where(low_lanes, turned, stats)
-    factor = jnp.exp(peaks - jnp.max(peaks, axis=0, keepdims=True))
-    factor = factor / jnp.sum(totals * factor, axis=0, keepdims=True)
-
-    wait_bytes(recv3, recv_sem.at[2])
-
-    context = jnp.sum(recv3[...] * factor, axis=0).astype(jnp.bfloat16)
-
-    ow_copy.wait()
-    if out_rows >= HD:
-        weight = ow[...]
-    else:
-        start = lax.rem(me * out_rows, HD)
-        row = lax.broadcasted_iota(jnp.int32, ow.shape, 0)
-        weight = jnp.where((row >= start) & (row < start + out_rows), ow[...].astype(jnp.float32), 0.0)
-        weight = weight.astype(jnp.bfloat16)
-    part = jnp.dot(context, weight, preferred_element_type=jnp.float32)
-    for c in range(chunks):
-        send4[c] = part[:, c * HD : (c + 1) * HD]
-
-    half = chunks // cores
-    remote(send4.at[pl.ds((1 - core) * half, half)], recv7, 6, me, 1 - core).start()
-    wait_bytes(recv7, recv_sem.at[6])
-    send7[...] = send4[pl.ds(core * half, half)] + recv7[...]
-
-    def send_part(c):
-        remote(send7.at[c], recv4.at[me], 3, c * spread, core).start()
-
-    each_other(my_head, heads, send_part)
-    to_either(first_is_here(), send7.at[my_head], recv4.at[me], 3, my_head * spread, core)
+    to_hub(me, is_hub, send3.at[my_head], recv3.at[core, me], 2)
+
+    @pl.when(is_hub)
+    def _():
+        wait_bytes(rows_in, recv_sem.at[6])
+        wait_bytes(recv6, recv_sem.at[5])
+        stats = recv6[...]
+        turned = pltpu.roll(stats, HD // 2, 3)
+        low_lanes = lax.broadcasted_iota(jnp.int32, stats.shape, 3) < HD // 2
+        peaks = jnp.where(low_lanes, stats, turned)
+        totals = jnp.where(low_lanes, turned, stats)
+        factor = jnp.exp(peaks - jnp.max(peaks, axis=1, keepdims=True))
+        factor = factor / jnp.sum(totals * factor, axis=1, keepdims=True)
+        rows = jnp.concatenate([rows_in[...].astype(jnp.bfloat16), output_rows()], axis=0)
+
+        wait_bytes(recv3, recv_sem.at[2])
+        context = jnp.sum(recv3[...] * factor, axis=1).astype(jnp.bfloat16)
+        context = jnp.concatenate([context[group] for group in range(groups)], axis=1)
+        part = jnp.dot(context, rows, preferred_element_type=jnp.float32)
+        for c in range(heads * per_head):
+            send4[c // per_head, c % per_head] = part[:, c * HD : (c + 1) * HD]
+
+        def send_part(h):
+            to_hub(h * spread, None, send4.at[h], recv4.at[me], 3)
+
+        each_other(my_head, heads, send_part)
+        here = None if spread == 1 else owner
+        if here is None:
+            local(send4.at[my_head], recv4.at[me], recv_sem.at[3]).start()
+        else:
+            to_hub(my_head * spread, here, send4.at[my_head], recv4.at[me], 3)
 
     def gather_out():
         wait_bytes(recv4, recv_sem.at[3])
         send5[...] = jnp.sum(recv4[...], axis=0)
 
         def send(other):
-            remote(send5, recv5.at[my_chunk], 4, other // cores, lax.rem(other, cores)).start()
-
-        each_other(me * cores + core, devices, send)
-        local(send5, recv5.at[my_chunk], recv_sem.at[4]).start()
+            for group in range(groups):
+                remote(send5, recv5.at[my_head], 4, other, group).start()
+
+        each_other(me, n, send)
+        for group in range(groups - 1):
+            remote(send5, recv5.at[my_head], 4, me, group).start()
+        local(send5, recv5.at[my_head], recv_sem.at[4]).start()
 
     when_owner(gather_out)
     wait_bytes(recv5, recv_sem.at[4])
-    for c in range(chunks):
-        out[:, c * HD : (c + 1) * HD] = recv5[c]
+    for c in range(heads * per_head):
+        out[:, c * HD : (c + 1) * HD] = recv5[c // per_head, c % per_head]
+
+    for phase, piece in ((2, recv3), (5, recv6)):
+        wait_bytes(piece.at[0, pl.ds(0, n - 1)], send_sem.at[phase])
+
+        @pl.when(jnp.logical_not(is_hub))
+        def _():
+            wait_bytes(piece.at[0, 0], send_sem.at[phase])
+
+    wait_bytes(send1.at[pl.ds(0, heads - 1)], send_sem.at[0])
+
+    @pl.when(jnp.logical_not(here))
+    def _():
+        wait_bytes(send1.at[0], send_sem.at[0])
+
+    @pl.when(jnp.logical_not(is_hub))
+    def _():
+        wait_bytes(rows_out, send_sem.at[6])
+
+    @pl.when(is_hub)
+    def _():
+        wait_bytes(send4.at[pl.ds(0, heads - 1)], send_sem.at[3])
+
+    if spread > 1:
+
+        @pl.when(is_hub & jnp.logical_not(owner))
+        def _():
+            wait_bytes(send4.at[0], send_sem.at[3])
 
     def owner_sends():
-        wait_bytes(send1.at[pl.ds(0, heads - 1)], send_sem.at[0])
-        wait_bytes(recv1.at[pl.ds(0, n - 1)], send_sem.at[1])
-        wait_bytes(send7.at[pl.ds(0, heads - 1)], send_sem.at[3])
-        if devices - 1 <= chunks:
-            wait_bytes(recv5.at[pl.ds(0, devices - 1)], send_sem.at[4])
-        else:
-            wait_bytes(recv4, send_sem.at[4])
+        for group in range(groups):
+            wait_bytes(recv1.at[group, pl.ds(0, n - 1)], send_sem.at[1])
             wait_bytes(recv4.at[pl.ds(0, n - 1)], send_sem.at[4])
+        for group in range(groups - 1):
+            wait_bytes(recv1.at[group, 0], send_sem.at[1])
+            wait_bytes(recv4.at[0], send_sem.at[4])
 
     when_owner(owner_sends)
-    if spread > 1:
-
-        @pl.when(jnp.logical_not(owner))
-        def _():
-            wait_bytes(send1, send_sem.at[0])
-            wait_bytes(send7, send_sem.at[3])
-
-    wait_bytes(recv3.at[pl.ds(0, n - 1)], send_sem.at[2])
-    wait_bytes(recv6.at[pl.ds(0, n - 1)], send_sem.at[5])
-    wait_bytes(recv7, send_sem.at[6])
 
 
 def body(
@@ -391,22 +416,22 @@
             vmem((batch, context_len, rank), bf16),
             vmem((max(out_weight.shape[1], HD), model), bf16),
             vmem((heads, batch, HD), f32),
-            vmem((n, batch, HD), f32),
-            vmem((batch, HD), f32),
+            vmem((cores, n, batch, HD), f32),
+            vmem((cores, batch, HD), f32),
             vmem((heads, batch, HD), f32),
             vmem((rank // HD, heads * batch, HD), f32),
             vmem((rank // HD, heads * batch, HD), f32),
             vmem((heads * batch, HD), f32),
             vmem((heads, batch, HD), f32),
-            vmem((n, batch, HD), f32),
-            vmem((chunks, batch, HD), f32),
-            vmem((n, batch, HD), f32),
-            vmem((batch, HD), f32),
-            vmem((chunks, batch, HD), f32),
+            vmem((cores, n, batch, HD), f32),
+            vmem((heads, chunks // heads, batch, HD), f32),
+            vmem((n, chunks // heads, batch, HD), f32),
+            vmem((chunks // heads, batch, HD), f32),
+            vmem((heads, chunks // heads, batch, HD), f32),
             vmem((heads, batch, HD), f32),
-            vmem((n, batch, HD), f32),
-            vmem((chunks // cores, batch, HD), f32),
-            vmem((chunks // cores, batch, HD), f32),
+            vmem((cores, n, batch, HD), f32),
+            vmem((max(out_weight.shape[1], HD), model), f32),
+            vmem((max(out_weight.shape[1], HD), model), f32),
             vmem((batch, 2 * heads, context_len), bf16),
             pltpu.SemaphoreType.DMA((7,)),
             pltpu.SemaphoreType.DMA((batch,)),

time: 33.7 us -> 32.6 us (0.967)
  Pallas kernels: 32.5 us -> 31.4 us
    pallas_call x1, Pallas kernels: 32.5 us -> 31.4 us  [body(): pl.pallas_call(functools.partial(kernel, n, cores), out_shape=pltpu.VMEM(...]
where the time goes in v4:
time: 32.6 us; the launch traced here: 32.1 us
  Pallas kernels  31.4 us (96%)
  local copies, waits for them, and re-layouts  0.66 us (2%)
    pallas_call x1, Pallas kernels, body(): pl.pallas_call(functools.partial(kernel, n, cores), out_shape=pltpu.VMEM(...  31.4 us
    unnamed x1, local copies, waits for them, and re-layouts  0.66 us

profile of v4, /device:TPU:1, one launch (start us, length us, event | category | flops | bytes accessed | tf_op | source)
XLA Modules:
  0.0 32.1 jit_solution(10784460306711418345)
XLA Ops:
  0.0 31.4 %shard_map.91 = f32[8,4096]{1,0:T(8,128)S(1)} custom-call(s32[8]{0:T(128)} %lengths_in.1, s32[4,8]{1,0:T(4,128)} %bitcast.13, bf16[8,4096]{1,0:T(8,128)(2,1)} %hidden_in.1, bf16[256,2048]{1,0:T(8,128)(2,1)} %bitcast.9, bf16[256,512]{1,0:T(8,128)(2,1)} %bitcast.11, bf16[256,512]{1,0:T(8,128)(2,1)} %bitcast.12, bf16[8,1024,256]{2,1,0:T(8,128)(2,1)} %bitcast.7, ...), custom_call_target="tpu_custom_call" | custom-call | tf_op jit(solution)/shard_map/pallas_call | solution.py:403
  31.4 0.7 %copy.11 = f32[8,4096]{1,0:T(8,128)} copy(f32[8,4096]{1,0:T(8,128)S(1)} %shard_map.91) | data formatting | bytes 262144

commit v5 on v4

--- a/solution.py
+++ b/solution.py
@@ -96,12 +96,14 @@
     batch, context_len = keys.shape[0], keys.shape[1]
     heads = KPG * REP
     spread = n // heads
-    my_head = me // spread
-    per_head = out.shape[1] // HD // heads
+    per_owner = send5.shape[0]
     hub = cores - 1
     groups = recv1.shape[0]
     dim_rows, out_rows = query_weight.shape[0], out_weight.shape[0]
-    owner = lax.rem(me, spread) == 0
+    owners, per = send1.shape[0], send1.shape[1]
+    first, stride = n // 4, n // 2 // owners
+    my_owner = lax.rem(me + n - first, n) // stride
+    owner = (me >= first) & (me < first + n // 2) & (lax.rem(me + n - first, stride) == 0)
     is_hub = core == hub
 
     def local(src, dst, sem):
@@ -121,7 +123,14 @@
         local(ref, ref, sem).wait()
 
     def when_owner(action):
-        pl.when(is_hub if spread == 1 else is_hub & owner)(action)
+        pl.when(is_hub & owner)(action)
+
+    def each_owner(step):
+        base = me * owners // n
+        flips = [(1 << b) * (1 - 2 * lax.rem(base // (1 << b), 2)) for b in range(owners.bit_length() - 1)]
+        for mask in reversed(range(owners)):
+            index = base + sum(flip for b, flip in enumerate(flips) if mask >> b & 1)
+            step(index, first + index * stride)
 
     def to_hub(other, own, src, dst, phase):
         if own is None:
@@ -196,16 +205,14 @@
         weight = weight.astype(jnp.bfloat16)
     part = jnp.dot(state, weight, preferred_element_type=jnp.float32)
     for h in range(heads):
-        send1[h] = part[:, h * HD : (h + 1) * HD]
+        send1[h // per, h % per] = part[:, h * HD : (h + 1) * HD]
 
     pl.semaphore_wait(barrier, devices - 1)
 
-    def send_query(h):
-        to_hub(h * spread, None, send1.at[h], recv1.at[core, me], 0)
-
-    each_other(my_head, heads, send_query)
-    here = is_hub if spread == 1 else is_hub & owner
-    to_hub(my_head * spread, here, send1.at[my_head], recv1.at[core, me], 0)
+    def send_query(index, chip):
+        to_hub(chip, is_hub & (chip == me), send1.at[index], recv1.at[core, me], 0)
+
+    each_owner(send_query)
 
     ow_copy.wait()
 
@@ -220,12 +227,12 @@
 
         def send(other):
             for group in range(groups):
-                remote(send2.at[group], recv2.at[my_head], 1, other, group).start()
+                remote(send2.at[group], recv2.at[my_owner], 1, other, group).start()
 
         each_other(me, n, send)
         for group in range(groups - 1):
-            remote(send2.at[group], recv2.at[my_head], 1, me, group).start()
-        local(send2.at[hub], recv2.at[my_head], recv_sem.at[1]).start()
+            remote(send2.at[group], recv2.at[my_owner], 1, me, group).start()
+        local(send2.at[hub], recv2.at[my_owner], recv_sem.at[1]).start()
 
     when_owner(gather_query)
     uk_copy.wait()
@@ -234,7 +241,7 @@
     scale = 1.0 / math.sqrt(HD)
     rank = uk.shape[0]
     for j in range(KPG):
-        rows = recv2[j * REP : (j + 1) * REP].reshape(REP * batch, HD)
+        rows = jnp.concatenate([recv2[h // per, h % per] for h in range(j * REP, (j + 1) * REP)], axis=0)
         mapped = folded(dot_nt(halves(rows), uk[:, j * HD : (j + 1) * HD])) * scale
         for k in range(rank // HD):
             ql[k, j * REP * batch : (j + 1) * REP * batch, :] = mapped[:, k * HD : (k + 1) * HD]
@@ -267,7 +274,7 @@
         to_hub(other, None, send6.at[other // spread], recv6.at[core, me], 5)
 
     each_other(me, n, send_stats)
-    to_hub(me, is_hub, send6.at[my_head], recv6.at[core, me], 5)
+    to_hub(me, is_hub, send6.at[me // spread], recv6.at[core, me], 5)
 
     for b in range(batch):
         value_copies[b].wait()
@@ -292,7 +299,7 @@
         to_hub(other, None, send3.at[other // spread], recv3.at[core, me], 2)
 
     each_other(me, n, send_carry)
-    to_hub(me, is_hub, send3.at[my_head], recv3.at[core, me], 2)
+    to_hub(me, is_hub, send3.at[me // spread], recv3.at[core, me], 2)
 
     @pl.when(is_hub)
     def _():
@@ -311,18 +318,13 @@
         context = jnp.sum(recv3[...] * factor, axis=1).astype(jnp.bfloat16)
         context = jnp.concatenate([context[group] for group in range(groups)], axis=1)
         part = jnp.dot(context, rows, preferred_element_type=jnp.float32)
-        for c in range(heads * per_head):
-            send4[c // per_head, c % per_head] = part[:, c * HD : (c + 1) * HD]
-
-        def send_part(h):
-            to_hub(h * spread, None, send4.at[h], recv4.at[me], 3)
-
-        each_other(my_head, heads, send_part)
-        here = None if spread == 1 else owner
-        if here is None:
-            local(send4.at[my_head], recv4.at[me], recv_sem.at[3]).start()
-        else:
-            to_hub(my_head * spread, here, send4.at[my_head], recv4.at[me], 3)
+        for c in range(owners * per_owner):
+            send4[c // per_owner, c % per_owner] = part[:, c * HD : (c + 1) * HD]
+
+        def send_part(index, chip):
+            to_hub(chip, chip == me, send4.at[index], recv4.at[me], 3)
+
+        each_owner(send_part)
 
     def gather_out():
         wait_bytes(recv4, recv_sem.at[3])
@@ -330,17 +332,17 @@
 
         def send(other):
             for group in range(groups):
-                remote(send5, recv5.at[my_head], 4, other, group).start()
+                remote(send5, recv5.at[my_owner], 4, other, group).start()
 
         each_other(me, n, send)
         for group in range(groups - 1):
-            remote(send5, recv5.at[my_head], 4, me, group).start()
-        local(send5, recv5.at[my_head], recv_sem.at[4]).start()
+            remote(send5, recv5.at[my_owner], 4, me, group).start()
+        local(send5, recv5.at[my_owner], recv_sem.at[4]).start()
 
     when_owner(gather_out)
     wait_bytes(recv5, recv_sem.at[4])
-    for c in range(heads * per_head):
-        out[:, c * HD : (c + 1) * HD] = recv5[c // per_head, c % per_head]
+    for c in range(owners * per_owner):
+        out[:, c * HD : (c + 1) * HD] = recv5[c // per_owner, c % per_owner]
 
     for phase, piece in ((2, recv3), (5, recv6)):
         wait_bytes(piece.at[0, pl.ds(0, n - 1)], send_sem.at[phase])
@@ -349,9 +351,9 @@
         def _():
             wait_bytes(piece.at[0, 0], send_sem.at[phase])
 
-    wait_bytes(send1.at[pl.ds(0, heads - 1)], send_sem.at[0])
-
-    @pl.when(jnp.logical_not(here))
+    wait_bytes(send1.at[pl.ds(0, owners - 1)], send_sem.at[0])
+
+    @pl.when(jnp.logical_not(is_hub & owner))
     def _():
         wait_bytes(send1.at[0], send_sem.at[0])
 
@@ -361,13 +363,11 @@
 
     @pl.when(is_hub)
     def _():
-        wait_bytes(send4.at[pl.ds(0, heads - 1)], send_sem.at[3])
-
-    if spread > 1:
-
-        @pl.when(is_hub & jnp.logical_not(owner))
-        def _():
-            wait_bytes(send4.at[0], send_sem.at[3])
+        wait_bytes(send4.at[pl.ds(0, owners - 1)], send_sem.at[3])
+
+    @pl.when(is_hub & jnp.logical_not(owner))
+    def _():
+        wait_bytes(send4.at[0], send_sem.at[3])
 
     def owner_sends():
         for group in range(groups):
@@ -398,6 +398,8 @@
     heads = KPG * REP
     model = out_weight.shape[2]
     chunks = model // HD
+    owners = min(heads, n // 2)
+    per = heads // owners
     f32, bf16 = jnp.float32, jnp.bfloat16
     vmem = pltpu.VMEM
     return pl.pallas_call(
@@ -415,19 +417,19 @@
             vmem((batch, context_len, rank), bf16),
             vmem((batch, context_len, rank), bf16),
             vmem((max(out_weight.shape[1], HD), model), bf16),
-            vmem((heads, batch, HD), f32),
-            vmem((cores, n, batch, HD), f32),
-            vmem((cores, batch, HD), f32),
-            vmem((heads, batch, HD), f32),
+            vmem((owners, per, batch, HD), f32),
+            vmem((cores, n, per, batch, HD), f32),
+            vmem((cores, per, batch, HD), f32),
+            vmem((owners, per, batch, HD), f32),
             vmem((rank // HD, heads * batch, HD), f32),
             vmem((rank // HD, heads * batch, HD), f32),
             vmem((heads * batch, HD), f32),
             vmem((heads, batch, HD), f32),
             vmem((cores, n, batch, HD), f32),
-            vmem((heads, chunks // heads, batch, HD), f32),
-            vmem((n, chunks // heads, batch, HD), f32),
-            vmem((chunks // heads, batch, HD), f32),
-            vmem((heads, chunks // heads, batch, HD), f32),
+            vmem((owners, chunks // owners, batch, HD), f32),
+            vmem((n, chunks // owners, batch, HD), f32),
+            vmem((chunks // owners, batch, HD), f32),
+            vmem((owners, chunks // owners, batch, HD), f32),
             vmem((heads, batch, HD), f32),
             vmem((cores, n, batch, HD), f32),
             vmem((max(out_weight.shape[1], HD), model), f32),

time: 32.6 us -> 32.2 us (0.988)
  Pallas kernels: 31.4 us -> 31 us
    pallas_call x1, Pallas kernels: 31.4 us -> 31 us  [body(): pl.pallas_call(functools.partial(kernel, n, cores), out_shape=pltpu.VMEM(...]
where the time goes in v5:
time: 32.2 us; the launch traced here: 31.7 us
  Pallas kernels  31 us (96%)
  local copies, waits for them, and re-layouts  0.66 us (2%)
    pallas_call x1, Pallas kernels, body(): pl.pallas_call(functools.partial(kernel, n, cores), out_shape=pltpu.VMEM(...  31 us
    unnamed x1, local copies, waits for them, and re-layouts  0.66 us

profile of v5, /device:TPU:1, one launch (start us, length us, event | category | flops | bytes accessed | tf_op | source)
XLA Modules:
  0.0 31.7 jit_solution(5643928882514231382)
XLA Ops:
  0.0 31.0 %shard_map.91 = f32[8,4096]{1,0:T(8,128)S(1)} custom-call(s32[8]{0:T(128)} %lengths_in.1, s32[4,8]{1,0:T(4,128)} %bitcast.13, bf16[8,4096]{1,0:T(8,128)(2,1)} %hidden_in.1, bf16[256,2048]{1,0:T(8,128)(2,1)} %bitcast.9, bf16[256,512]{1,0:T(8,128)(2,1)} %bitcast.11, bf16[256,512]{1,0:T(8,128)(2,1)} %bitcast.12, bf16[8,1024,256]{2,1,0:T(8,128)(2,1)} %bitcast.7, ...), custom_call_target="tpu_custom_call" | custom-call | tf_op jit(solution)/shard_map/pallas_call | solution.py:405
  31.0 0.7 %copy.11 = f32[8,4096]{1,0:T(8,128)} copy(f32[8,4096]{1,0:T(8,128)S(1)} %shard_map.91) | data formatting | bytes 262144

commit v6 on v5

--- a/solution.py
+++ b/solution.py
@@ -330,11 +330,14 @@
         wait_bytes(recv4, recv_sem.at[3])
         send5[...] = jnp.sum(recv4[...], axis=0)
 
-        def send(other):
-            for group in range(groups):
+        def send_to(group):
+            def send(other):
                 remote(send5, recv5.at[my_owner], 4, other, group).start()
 
-        each_other(me, n, send)
+            return send
+
+        for group in range(groups):
+            each_other(me, n, send_to(group))
         for group in range(groups - 1):
             remote(send5, recv5.at[my_owner], 4, me, group).start()
         local(send5, recv5.at[my_owner], recv_sem.at[4]).start()

time: 32.2 us -> 31.9 us (level); the launches traced: 31.7 us -> 31.8 us
  no operation moved by 1% of the time
where the time goes in v6:
time: 31.9 us; the launch traced here: 31.8 us
  Pallas kernels  31.1 us (97%)
  local copies, waits for them, and re-layouts  0.66 us (2%)
    pallas_call x1, Pallas kernels, body(): pl.pallas_call(functools.partial(kernel, n, cores), out_shape=pltpu.VMEM(...  31.1 us
    unnamed x1, local copies, waits for them, and re-layouts  0.66 us

profile of v6, /device:TPU:1, one launch (start us, length us, event | category | flops | bytes accessed | tf_op | source)
XLA Modules:
  0.0 31.8 jit_solution(1412095527393276477)
XLA Ops:
  0.0 31.1 %shard_map.91 = f32[8,4096]{1,0:T(8,128)S(1)} custom-call(s32[8]{0:T(128)} %lengths_in.1, s32[4,8]{1,0:T(4,128)} %bitcast.13, bf16[8,4096]{1,0:T(8,128)(2,1)} %hidden_in.1, bf16[256,2048]{1,0:T(8,128)(2,1)} %bitcast.9, bf16[256,512]{1,0:T(8,128)(2,1)} %bitcast.11, bf16[256,512]{1,0:T(8,128)(2,1)} %bitcast.12, bf16[8,1024,256]{2,1,0:T(8,128)(2,1)} %bitcast.7, ...), custom_call_target="tpu_custom_call" | custom-call | tf_op jit(solution)/shard_map/pallas_call | solution.py:408
  31.1 0.7 %copy.11 = f32[8,4096]{1,0:T(8,128)} copy(f32[8,4096]{1,0:T(8,128)S(1)} %shard_map.91) | data formatting | bytes 262144
